TPU v7x, 32 devices: a whole 2x2x4 slice. The times are simulated.
32 devices in a mesh: dp: 8 (over z, core), seq: 4 (over y, x).
Axes of the slice: x: 2, y: 2, z: 4, core: 2. Of those that a mesh axis runs over, the one named last changes fastest.
Arguments:
- tokens: bfloat16 [32, 256, 1024], P(('dp', 'seq')), may hold values from -6 to 6
- queries: bfloat16 [32, 256, 1024], P(('dp', 'seq')), may hold values from -240 to 240
- keys: bfloat16 [32, 256, 1024], P(('dp', 'seq')), may hold values from -7 to 7
- values: bfloat16 [32, 256, 1024], P(('dp', 'seq')), may hold values from -6 to 6
- ln_gain: bfloat16 [1024], replicated, may hold values from 0.5 to 1.5
- mean_in: bfloat16 [1024, 2048], P(None, 'seq'), may hold values from -0.1875 to 0.1875
- sigma_in: bfloat16 [1024, 2048], P(None, 'seq'), may hold values from 0.0039978027 to 0.029907227
- noise_in: bfloat16 [1024, 2048], P(None, 'seq'), may hold values from -4 to 4
- mean_out: bfloat16 [2048, 1024], P('seq'), may hold values from -0.125 to 0.125
- sigma_out: bfloat16 [2048, 1024], P('seq'), may hold values from 0.0019989014 to 0.014953613
- noise_out: bfloat16 [2048, 1024], P('seq'), may hold values from -4 to 4
- flip_in: int32 [32, 1024], P('dp'), may hold values from -1 to 1, as said below
- flip_mid: int32 [32, 2048], P('dp', 'seq'), may hold values from -1 to 1, as said below
- flip_hidden: int32 [32, 2048], P('dp', 'seq'), may hold values from -1 to 1, as said below
- flip_out: int32 [32, 1024], P('dp'), may hold values from -1 to 1, as said below
- cotangent: bfloat16 [32, 256, 1024], P(('dp', 'seq')), may hold values from -0.75 to 0.75
Outputs:
- block_out: bfloat16 [32, 256, 1024], P(('dp', 'seq'))
- resid_grad: bfloat16 [32, 256, 1024], P(('dp', 'seq'))
- grad_mean_in: float32 [1024, 2048], P(None, 'seq')
- grad_sigma_in: float32 [1024, 2048], P(None, 'seq')
- grad_mean_out: float32 [2048, 1024], P('seq')
- grad_sigma_out: float32 [2048, 1024], P('seq')
Inputs may be any that keep to these rules, and one draw needn't show every extreme that they name: `flip_in`: each entry is -1 or +1. `flip_mid`: each entry is -1 or +1. `flip_hidden`: each entry is -1 or +1. `flip_out`: each entry is -1 or +1.
All inputs are finite; a program needn't handle non-finite values.
Results may differ from a plain program's by a relative error of at most 0.018.
Values may be sent and summed in bfloat16 or wider, within the bound.
A program may use at most 128 MiB of HBM per device.

v0:
```python
import jax
import jax.numpy as jnp
from jax import lax
from jax.sharding import PartitionSpec as P

HEADS = 16


def gelu_slope(pre):
    cdf = 0.5 * (1.0 + lax.erf(pre * 0.7071067811865476))
    pdf = jnp.exp(-0.5 * pre * pre) * 0.3989422804014327
    return cdf + pre * pdf


def contract_first(left, right):
    return lax.dot_general(
        left, right, (((0,), (0,)), ((), ())), preferred_element_type=jnp.float32
    )


def contract_last(left, right):
    return lax.dot_general(
        left, right, (((1,), (1,)), ((), ())), preferred_element_type=jnp.float32
    )


def body(
    tokens,
    queries,
    keys,
    values,
    ln_gain,
    mean_in,
    sigma_in,
    noise_in,
    mean_out,
    sigma_out,
    noise_out,
    flip_in,
    flip_mid,
    flip_hidden,
    flip_out,
    cotangent,
):
    bf = jnp.bfloat16
    f32 = jnp.float32
    own_images, patches, width = tokens.shape
    hidden_local = mean_in.shape[1]
    head_dim = width // HEADS
    scale = head_dim ** (-0.5)
    pert_in = (sigma_in.astype(f32) * noise_in.astype(f32)).astype(bf)
    pert_out = (sigma_out.astype(f32) * noise_out.astype(f32)).astype(bf)
    query_heads = queries.reshape(own_images, patches, HEADS, head_dim)
    key_heads = keys.reshape(own_images, patches, HEADS, head_dim)
    value_heads = values.reshape(own_images, patches, HEADS, head_dim)
    scores = (
        jnp.einsum("bqhe,bkhe->bhqk", query_heads, key_heads, preferred_element_type=f32) * scale
    )
    top = jnp.max(scores, axis=-1, keepdims=True)
    expd = jnp.exp(scores - top)
    total = jnp.sum(expd, axis=-1)
    accum = jnp.einsum("bhqk,bkhe->bqhe", expd.astype(bf), value_heads, preferred_element_type=f32)
    attn_out = (
        (accum / jnp.transpose(total, (0, 2, 1))[..., None])
        .reshape(own_images, patches, width)
        .astype(bf)
    )
    resid = (tokens.astype(f32) + attn_out.astype(f32)).astype(bf)
    resid_f = resid.astype(f32)
    centered = resid_f - jnp.mean(resid_f, axis=-1, keepdims=True)
    rstd = lax.rsqrt(jnp.mean(centered * centered, axis=-1, keepdims=True) + 1e-06)
    ahat = centered * rstd
    gain_f = ln_gain.astype(f32)
    normed = (ahat * gain_f).astype(bf)
    in_signs = flip_in.astype(bf)[:, None, :]
    in_signs_f = flip_in.astype(f32)[:, None, :]
    mid_signs = flip_mid.astype(bf)[:, None, :]
    mid_signs_f = flip_mid.astype(f32)[:, None, :]
    hid_signs = flip_hidden.astype(bf)[:, None, :]
    hid_signs_f = flip_hidden.astype(f32)[:, None, :]
    out_signs = flip_out.astype(bf)[:, None, :]
    out_signs_f = flip_out.astype(f32)[:, None, :]
    gathered = lax.all_gather(normed, "seq", axis=0, tiled=True)
    count = gathered.shape[0]
    signs = in_signs
    flat = gathered.reshape(-1, width)
    flat_flip = (gathered * signs).reshape(-1, width)
    plain = jnp.dot(flat, mean_in, preferred_element_type=f32).reshape(count, patches, hidden_local)
    noisy = jnp.dot(flat_flip, pert_in, preferred_element_type=f32).reshape(
        count, patches, hidden_local
    )
    pre = plain + noisy * mid_signs_f
    group_images = pre.shape[0]
    rows = group_images * patches
    hidden = jax.nn.gelu(pre, approximate=False).astype(bf)
    flipped_hidden = hidden * hid_signs
    count = lax.axis_size("seq") * own_images
    hb = hidden.reshape(-1, hidden_local)
    hfb = flipped_hidden.reshape(-1, hidden_local)
    plain = jnp.dot(hb, mean_out, preferred_element_type=f32).reshape(count, patches, width)
    noisy = jnp.dot(hfb, pert_out, preferred_element_type=f32).reshape(count, patches, width)
    mixed = lax.psum_scatter(
        (plain + noisy * out_signs_f).astype(jnp.bfloat16), "seq", scatter_dimension=0, tiled=True
    ).astype(jnp.float32)
    block_out = (resid_f + mixed).astype(bf)
    cot_all = lax.all_gather(cotangent, "seq", axis=0, tiled=True)
    cot_flat = cot_all.reshape(rows, width)
    cot_flip_flat = (cot_all * out_signs).reshape(rows, width)
    dhidden = contract_last(cot_flat, mean_out).reshape(group_images, patches, hidden_local)
    dhidden = (
        dhidden
        + contract_last(cot_flip_flat, pert_out).reshape(group_images, patches, hidden_local)
        * hid_signs_f
    )
    dpre = (dhidden * gelu_slope(pre)).astype(bf)
    dpre_flip = dpre * mid_signs
    local_mean_out = contract_first(hidden.reshape(rows, hidden_local), cot_flat)
    local_sigma_out = contract_first(
        flipped_hidden.reshape(rows, hidden_local), cot_flip_flat
    ) * noise_out.astype(f32)
    grad_mean_out, grad_sigma_out = (
        lax.psum(local_mean_out.astype(jnp.bfloat16), "dp").astype(jnp.float32),
        lax.psum(local_sigma_out.astype(jnp.bfloat16), "dp").astype(jnp.float32),
    )
    local_mean_in = contract_first(gathered.reshape(rows, width), dpre.reshape(rows, hidden_local))
    local_flip_in = contract_first(
        (gathered * in_signs).reshape(rows, width), dpre_flip.reshape(rows, hidden_local)
    )
    local_sigma_in = local_flip_in * noise_in.astype(f32)
    count = lax.axis_size("seq") * own_images
    drows = dpre.reshape(-1, hidden_local)
    dflip_rows = dpre_flip.reshape(-1, hidden_local)
    signs = in_signs_f
    plain = contract_last(drows, mean_in).reshape(count, patches, width)
    noisy = contract_last(dflip_rows, pert_in).reshape(count, patches, width)
    dnormed = lax.psum_scatter(
        (plain + noisy * signs).astype(jnp.bfloat16), "seq", scatter_dimension=0, tiled=True
    ).astype(jnp.float32)
    grad_mean_in, grad_sigma_in = (
        lax.psum(local_mean_in.astype(jnp.bfloat16), "dp").astype(jnp.float32),
        lax.psum(local_sigma_in.astype(jnp.bfloat16), "dp").astype(jnp.float32),
    )
    scaled = dnormed * gain_f
    back = rstd * (
        scaled
        - jnp.mean(scaled, axis=-1, keepdims=True)
        - ahat * jnp.mean(scaled * ahat, axis=-1, keepdims=True)
    )
    resid_grad = (cotangent.astype(f32) + back).astype(bf)
    return (block_out, resid_grad, grad_mean_in, grad_sigma_in, grad_mean_out, grad_sigma_out)


def solution(mesh):
    return jax.shard_map(
        body,
        mesh=mesh,
        in_specs=(
            P(("dp", "seq"), None, None),
            P(("dp", "seq"), None, None),
            P(("dp", "seq"), None, None),
            P(("dp", "seq"), None, None),
            P(),
            P(None, "seq"),
            P(None, "seq"),
            P(None, "seq"),
            P("seq", None),
            P("seq", None),
            P("seq", None),
            P("dp", None),
            P("dp", "seq"),
            P("dp", "seq"),
            P("dp", None),
            P(("dp", "seq"), None, None),
        ),
        out_specs=(
            P(("dp", "seq"), None, None),
            P(("dp", "seq"), None, None),
            P(None, "seq"),
            P(None, "seq"),
            P("seq", None),
            P("seq", None),
        ),
        check_vma=False,
    )
```

profile of v0, /device:TPU:0, one launch (start us, length us, event | category | flops | bytes accessed | tf_op | source)
XLA Modules:
  0.0 289.0 jit_solution(1723222755347720097)
XLA Ops:
  13.9 1.5 convert_reduce_fusion
  18.0 37.0 %all-gather.3.cloned.1.call-done = bf16[4,256,1024]{2,1,0:T(8,128)(2,1)} async-done(((bf16[1,256,1024]{2,1,0:T(8,128)(2,1)}), bf16[4,256,1024]{2,1,0:T(8,128)(2,1)}) %all-gather.3.cloned.1.call-update) | async-done | bytes 2097168 | tf_op jit(solution)/shard_map/all_gather | solution.py:83
  55.0 3.3 %fusion.31 = f32[4,256,512]{2,1,0:T(8,128)S(1)} fusion(bf16[4,256,1024]{2,1,0:T(8,128)(2,1)} %all-gather.3.cloned.1.call-done, bf16[4,1024]{1,0:T(4,128)(2,1)S(1)} %get-tuple-element.19, bf16[1024,512]{1,0:T(8,128)(2,1)S(1)} %copy-done.7, bf16[1024,512]{1,0:T(8,128)(2,1)} %param.22), kind=kOutput, calls=%fused_computation.55 | convolution fusion | flops 1076887552 | bytes 6299648 | tf_op jit(solution)/shard_map/dot_general | solution.py:89
  58.3 1.9 fusion.77
  61.5 4.7 %fusion.8 = bf16[4,256,512]{2,1,0:T(8,128)(2,1)S(1)} fusion(f32[4,256,512]{2,1,0:T(8,128)S(1)} %get-tuple-element.28, u8[256,512]{1,0:T(8,128)(4,1)S(1)} %get-tuple-element.7, u8[256,512]{1,0:T(8,128)(4,1)S(1)} %get-tuple-element.6), kind=kLoop, calls=%fused_computation.18 | loop fusion | flops 36700160 | bytes 3407872 | tf_op jit(solution)/shard_map/convert_element_type | solution.py:95
  66.2 25.8 %all-gather.5.cloned.1.call-done = bf16[4,256,1024]{2,1,0:T(8,128)(2,1)} async-done(((bf16[1,256,1024]{2,1,0:T(8,128)(2,1)}), bf16[4,256,1024]{2,1,0:T(8,128)(2,1)}) %all-gather.5.cloned.1.call-update) | async-done | bytes 2097168 | tf_op jit(solution)/shard_map/all_gather | solution.py:106
  92.0 3.6 %fusion.27 = f32[4,256,512]{2,1,0:T(8,128)S(1)} fusion(bf16[4,256,1024]{2,1,0:T(8,128)(2,1)} %all-gather.5.cloned.1.call-done, bf16[4,1024]{1,0:T(4,128)(2,1)S(1)} %get-tuple-element.20, bf16[512,1024]{1,0:T(8,128)(2,1)} %param.26, bf16[512,1024]{1,0:T(8,128)(2,1)} %param.25), kind=kOutput, calls=%fused_computation.51 | convolution fusion | flops 1076887552 | bytes 6299648 | tf_op jit(solution)/shard_map/dot_general | solution.py:22
  95.8 2.0 fusion.14
  97.8 2.3 bitcast_convert_fusion.1
  100.1 2.3 fusion.3
  102.4 2.3 bitcast_convert_fusion
  104.6 2.4 fusion.5
  107.3 2.7 fusion.58
  110.0 2.6 add_convert_fusion
  112.7 2.6 fusion.56
  115.4 2.6 add_convert_fusion.1
  118.0 85.7 %all-reduce.5.cloned.1.call-done = (bf16[1024,512]{1,0:T(8,128)(2,1)}, bf16[1024,512]{1,0:T(8,128)(2,1)}, bf16[512,1024]{1,0:T(8,128)(2,1)}, bf16[512,1024]{1,0:T(8,128)(2,1)}) async-done(((bf16[1024,512]{1,0:T(8,128)(2,1)}, bf16[1024,512]{1,0:T(8,128)(2,1)}, bf16[512,1024]{1,0:T(8,128)(2,1)}, bf16[512,1024]{1,0:T(8,128)(2,1)}), (bf16[1024,512]{1,0:T(8,128)(2,1)}, bf16[1024,512]{1,0:T(8,128)(2,1)}, ...) | async-done | bytes 4194320 | tf_op jit(solution)/shard_map/psum | solution.py:140
  203.7 2.9 %convert_element_type.173 = f32[1024,512]{1,0:T(8,128)} convert(bf16[1024,512]{1,0:T(8,128)(2,1)} %get-tuple-element.10) | non-fusion elementwise | flops 524288 | bytes 3145728 | tf_op jit(solution)/shard_map/convert_element_type | solution.py:140
  206.7 1.6 convert_element_type.175
  208.3 1.6 convert_element_type.177
  209.8 1.6 convert_element_type.179
  211.4 30.4 %reduce-scatter.9.cloned.1.call-done = bf16[1,256,1024]{2,1,0:T(8,128)(2,1)} async-done(((bf16[4,256,1024]{2,1,0:T(8,128)(2,1)}), bf16[1,256,1024]{2,1,0:T(8,128)(2,1)}) %reduce-scatter.9.cloned.1.call-update) | async-done | bytes 524304
  243.2 36.6 %reduce-scatter.7.cloned.1.call-done = bf16[1,256,1024]{2,1,0:T(8,128)(2,1)} async-done(((bf16[4,256,1024]{2,1,0:T(8,128)(2,1)}), bf16[1,256,1024]{2,1,0:T(8,128)(2,1)}) %reduce-scatter.7.cloned.1.call-update) | async-done | bytes 524304
  279.8 2.6 fusion.50
  (83 shorter events, 12.3 us)
Async XLA Ops:
  7.2 51.1 %copy-start = (bf16[1024,512]{1,0:T(8,128)(2,1)S(1)}, bf16[1024,512]{1,0:T(8,128)(2,1)}, u32[]{:S(2)}) copy-start(bf16[1024,512]{1,0:T(8,128)(2,1)} %param.21) | copy-start | bytes 3145732
  7.2 2.7 copy-start.18
  7.2 47.8 %all-gather.3.cloned.1.call-start = ((), (), s32[]{:S(2)}) async-start(), calls=%async_computation.2 | async-start | bytes 2621440 | tf_op jit(solution)/shard_map/all_gather | solution.py:83
  13.9 4.0 %copy-start.22 = (s32[4,512]{1,0:T(4,128)S(1)}, s32[4,512]{1,0:T(4,128)}, u32[]{:S(2)}) copy-start(s32[4,512]{1,0:T(4,128)} %param.28) | copy-start | bytes 24580
  13.9 4.0 %copy-start.23 = (s32[4,512]{1,0:T(4,128)S(1)}, s32[4,512]{1,0:T(4,128)}, u32[]{:S(2)}) copy-start(s32[4,512]{1,0:T(4,128)} %param.29) | copy-start | bytes 24580
  13.9 4.0 %copy-start.20 = (s32[4,1024]{1,0:T(4,128)S(1)}, s32[4,1024]{1,0:T(4,128)}, u32[]{:S(2)}) copy-start(s32[4,1024]{1,0:T(4,128)} %param.27) | copy-start | bytes 49156
  13.9 4.0 %copy-start.21 = (s32[4,1024]{1,0:T(4,128)S(1)}, s32[4,1024]{1,0:T(4,128)}, u32[]{:S(2)}) copy-start(s32[4,1024]{1,0:T(4,128)} %param.30) | copy-start | bytes 49156
  13.9 41.0 %copy-start.7 = (bf16[1024,512]{1,0:T(8,128)(2,1)S(1)}, bf16[1024,512]{1,0:T(8,128)(2,1)}, u32[]{:S(2)}) copy-start(bf16[1024,512]{1,0:T(8,128)(2,1)} %param.23) | copy-start | bytes 3145732
  16.9 75.1 %all-gather.5.cloned.1.call-start = ((), (), s32[]{:S(2)}) async-start(), calls=%async_computation.3 | async-start | bytes 2621440 | tf_op jit(solution)/shard_map/all_gather | solution.py:106
  17.6 186.1 %all-reduce.5.cloned.1.call-start = ((), (), s32[]{:S(2)}) async-start(), calls=%async_computation.6 | async-start | bytes 8388608 | tf_op jit(solution)/shard_map/psum | solution.py:140
  55.0 3.3 %copy-start.25 = (bf16[4,256,1024]{2,1,0:T(8,128)(2,1)S(1)}, bf16[4,256,1024]{2,1,0:T(8,128)(2,1)}, u32[]{:S(2)}) copy-start(bf16[4,256,1024]{2,1,0:T(8,128)(2,1)} %all-gather.3.cloned.1.call-done) | copy-start | bytes 6291460
  92.0 3.6 %copy-start.3 = (bf16[4,256,1024]{2,1,0:T(8,128)(2,1)S(1)}, bf16[4,256,1024]{2,1,0:T(8,128)(2,1)}, u32[]{:S(2)}) copy-start(bf16[4,256,1024]{2,1,0:T(8,128)(2,1)} %all-gather.5.cloned.1.call-done) | copy-start | bytes 6291460
  92.0 3.6 %copy-start.5 = (f32[4,256,512]{2,1,0:T(8,128)S(1)}, f32[4,256,512]{2,1,0:T(8,128)}, u32[]{:S(2)}) copy-start(f32[4,256,512]{2,1,0:T(8,128)} %copy-done.4) | copy-start | bytes 6291460
  92.0 3.7 %copy-start.17 = (bf16[512,1024]{1,0:T(8,128)(2,1)S(1)}, bf16[512,1024]{1,0:T(8,128)(2,1)}, u32[]{:S(2)}) copy-start(bf16[512,1024]{1,0:T(8,128)(2,1)} %param.24) | copy-start | bytes 3145732
  97.8 2.3 copy-start.1
  107.0 134.8 %reduce-scatter.9.cloned.1.call-start = ((), (), s32[]{:S(2)}) async-start(), calls=%async_computation.5 | async-start | bytes 2621440
  107.3 2.7 copy-start.2
  107.3 2.7 copy-start.9
  107.3 2.7 copy-start.10
  112.7 167.2 %reduce-scatter.7.cloned.1.call-start = ((), (), s32[]{:S(2)}) async-start(), calls=%async_computation.4 | async-start | bytes 2621440
  112.7 2.7 copy-start.12
  112.7 2.7 copy-start.13
  203.7 2.9 %copy-start.16 = (bf16[1024,512]{1,0:T(8,128)(2,1)S(1)}, bf16[1024,512]{1,0:T(8,128)(2,1)}, u32[]{:S(2)}) copy-start(bf16[1024,512]{1,0:T(8,128)(2,1)} %get-tuple-element.11) | copy-start | bytes 3145732
  209.8 70.0 %copy-start.6 = (bf16[1,256,1024]{2,1,0:T(8,128)(2,1)S(1)}, bf16[1,256,1024]{2,1,0:T(8,128)(2,1)}, u32[]{:S(2)}) copy-start(bf16[1,256,1024]{2,1,0:T(8,128)(2,1)} %param.31) | copy-start | bytes 1572868
  (8 other events, 14.0 us)
Sparse Core Ops, SparseCore 0:
  17.0 37.8 all-gather.2
  56.8 35.1 all-gather.4
  107.1 96.5 all-reduce.4
  206.5 35.2 reduce-scatter.8
  244.6 35.1 reduce-scatter.6
where the time goes:
time: 289 us
  waiting for transfers between devices  216 us (75%)
  matrix products  32.2 us (11%)
  other arithmetic  20.2 us (7%)
  between operations  14.2 us (5%)
  local copies, waits for them, and re-layouts  5.66 us (2%)
    psum x1, waiting for transfers between devices, body(): lax.psum(local_mean_in.astype(jnp.bfloat16), 'dp').astype(jnp.float32)  85.7 us
    unnamed x7, waiting for transfers between devices  67.8 us
    all_gather x1, waiting for transfers between devices, body(): gathered = lax.all_gather(normed, 'seq', axis=0, tiled=True)  37 us
    all_gather x1, waiting for transfers between devices, body(): cot_all = lax.all_gather(cotangent, 'seq', axis=0, tiled=True)  25.8 us
    dot_general x4, matrix products, contract_last(): lax.dot_general(left, right, (((1,), (1,)), ((), ())), preferred_element_...  11 us
    dot_general x4, matrix products, contract_first(): lax.dot_general(left, right, (((0,), (0,)), ((), ())), preferred_element_...  9.14 us
  transfers between devices with their start and end apart: 5, of which 5 were waited for; matrix products, arithmetic and copies ran while one was open for 10% of the time, Pallas kernels for 0%

commit v1 on v0

--- a/solution.py
+++ b/solution.py
@@ -137,7 +137,9 @@
         (plain + noisy * signs).astype(jnp.bfloat16), "seq", scatter_dimension=0, tiled=True
     ).astype(jnp.float32)
     grad_mean_in, grad_sigma_in = (
-        lax.psum(local_mean_in.astype(jnp.bfloat16), "dp").astype(jnp.float32),
+        jnp.sum(lax.all_gather(local_mean_in.astype(jnp.bfloat16), "dp"), axis=0).astype(
+            jnp.float32
+        ),
         lax.psum(local_sigma_in.astype(jnp.bfloat16), "dp").astype(jnp.float32),
     )
     scaled = dnormed * gain_f

time: 289 us -> 356 us (1.23)
  waiting for transfers between devices: 216 us -> 274 us
  other arithmetic: 20.2 us -> 25.4 us
    all_gather x0 -> x1, waiting for transfers between devices: none -> 80.9 us  [body(): lax.all_gather(local_mean_in.astype(jnp.bfloat16), 'dp')]
    psum x1, waiting for transfers between devices: 85.7 us -> 60.8 us  [body(): lax.psum(local_sigma_in.astype(jnp.bfloat16), 'dp').astype(jnp.float32)]
    reduce_sum x0 -> x1, other arithmetic: none -> 5.24 us  [body(): jnp.sum(lax.all_gather(local_mean_in.astype(jnp.bfloat16), 'dp'), axis=0)]
    unnamed x7 -> x8, waiting for transfers between devices: 67.8 us -> 70 us
  transfers between devices with their start and end apart: 5 -> 6, of which waited for: 5 -> 6; matrix products, arithmetic and copies ran while one was open for 10% -> 10% of each run, Pallas kernels for 0% -> 0%
where the time goes in v1:
time: 356 us
  waiting for transfers between devices  274 us (77%)
  matrix products  33.2 us (9%)
  other arithmetic  25.4 us (7%)
  between operations  14.5 us (4%)
  local copies, waits for them, and re-layouts  7.7 us (2%)
    all_gather x1, waiting for transfers between devices, body(): lax.all_gather(local_mean_in.astype(jnp.bfloat16), 'dp')  80.9 us
    unnamed x8, waiting for transfers between devices  70 us
    psum x1, waiting for transfers between devices, body(): lax.psum(local_sigma_in.astype(jnp.bfloat16), 'dp').astype(jnp.float32)  60.8 us
    all_gather x1, waiting for transfers between devices, body(): gathered = lax.all_gather(normed, 'seq', axis=0, tiled=True)  37 us
    all_gather x1, waiting for transfers between devices, body(): cot_all = lax.all_gather(cotangent, 'seq', axis=0, tiled=True)  25.8 us
    dot_general x4, matrix products, contract_first(): lax.dot_general(left, right, (((0,), (0,)), ((), ())), preferred_element_...  12.4 us
    dot_general x4, matrix products, contract_last(): lax.dot_general(left, right, (((1,), (1,)), ((), ())), preferred_element_...  8.64 us
  transfers between devices with their start and end apart: 6, of which 6 were waited for; matrix products, arithmetic and copies ran while one was open for 10% of the time, Pallas kernels for 0%

profile of v1, /device:TPU:0, one launch (start us, length us, event | category | flops | bytes accessed | tf_op | source)
XLA Modules:
  0.0 355.9 jit_solution(1733378226351158116)
XLA Ops:
  18.0 37.0 %all-gather.5.cloned.1.call-done = bf16[4,256,1024]{2,1,0:T(8,128)(2,1)} async-done(((bf16[1,256,1024]{2,1,0:T(8,128)(2,1)}), bf16[4,256,1024]{2,1,0:T(8,128)(2,1)}) %all-gather.5.cloned.1.call-update) | async-done | bytes 2097168 | tf_op jit(solution)/shard_map/all_gather | solution.py:83
  55.0 3.3 fusion.31
  58.3 1.9 fusion.77
  61.5 4.7 %fusion.8 = bf16[4,256,512]{2,1,0:T(8,128)(2,1)S(1)} fusion(f32[4,256,512]{2,1,0:T(8,128)S(1)} %get-tuple-element.27, u8[256,512]{1,0:T(8,128)(4,1)S(1)} %get-tuple-element.7, u8[256,512]{1,0:T(8,128)(4,1)S(1)} %get-tuple-element.6), kind=kLoop, calls=%fused_computation.18 | loop fusion | flops 36700160 | bytes 3407872 | tf_op jit(solution)/shard_map/convert_element_type | solution.py:95
  66.2 25.8 %all-gather.7.cloned.1.call-done = bf16[4,256,1024]{2,1,0:T(8,128)(2,1)} async-done(((bf16[1,256,1024]{2,1,0:T(8,128)(2,1)}), bf16[4,256,1024]{2,1,0:T(8,128)(2,1)}) %all-gather.7.cloned.1.call-update) | async-done | bytes 2097168 | tf_op jit(solution)/shard_map/all_gather | solution.py:106
  92.0 4.0 %bitcast_convert_fusion = bf16[512,1024]{1,0:T(8,128)(2,1)} fusion(bf16[4,256,512]{2,1,0:T(8,128)(2,1)S(1)} %fusion.8, bf16[4,256,1024]{2,1,0:T(8,128)(2,1)} %all-gather.7.cloned.1.call-done), kind=kOutput, calls=%fused_computation.31 | convolution fusion | flops 1074266112 | bytes 4194304 | tf_op jit(solution)/shard_map/dot_general | solution.py:16
  97.3 2.3 fusion.5
  99.6 2.1 fusion.14
  102.7 2.3 fusion.3
  105.3 2.7 fusion.58
  108.0 2.6 add_convert_fusion
  110.7 2.6 fusion.56
  113.3 2.7 add_convert_fusion.1
  117.3 3.9 %bitcast_convert_fusion.1 = bf16[1024,512]{1,0:T(8,128)(2,1)} fusion(bf16[4,256,1024]{2,1,0:T(8,128)(2,1)} %all-gather.5.cloned.1.call-done, bf16[4,256,512]{2,1,0:T(8,128)(2,1)S(1)} %copy-done.3), kind=kOutput, calls=%fused_computation.32 | convolution fusion | flops 1074266112 | bytes 4194304 | tf_op jit(solution)/shard_map/dot_general | solution.py:16
  121.2 60.8 %all-reduce.5.cloned.1.call-done = (bf16[1024,512]{1,0:T(8,128)(2,1)}, bf16[512,1024]{1,0:T(8,128)(2,1)}, bf16[512,1024]{1,0:T(8,128)(2,1)}) async-done(((bf16[1024,512]{1,0:T(8,128)(2,1)}, bf16[512,1024]{1,0:T(8,128)(2,1)}, bf16[512,1024]{1,0:T(8,128)(2,1)}), (bf16[1024,512]{1,0:T(8,128)(2,1)}, bf16[512,1024]{1,0:T(8,128)(2,1)}, bf16[512,1024]{1,0:T(8,128)(2,1)})) %all-reduce.5.cloned.1.call-update) | async-done | bytes 3145744 | tf_op jit(solution)/shard_map/psum | solution.py:143
  182.0 2.9 convert_element_type.177
  184.9 1.6 convert_element_type.179
  186.5 1.6 convert_element_type.181
  188.0 32.5 %reduce-scatter.9.cloned.1.call-done = bf16[1,256,1024]{2,1,0:T(8,128)(2,1)} async-done(((bf16[4,256,1024]{2,1,0:T(8,128)(2,1)}), bf16[1,256,1024]{2,1,0:T(8,128)(2,1)}) %reduce-scatter.9.cloned.1.call-update) | async-done | bytes 524304
  222.0 36.6 %reduce-scatter.7.cloned.1.call-done = bf16[1,256,1024]{2,1,0:T(8,128)(2,1)} async-done(((bf16[4,256,1024]{2,1,0:T(8,128)(2,1)}), bf16[1,256,1024]{2,1,0:T(8,128)(2,1)}) %reduce-scatter.7.cloned.1.call-update) | async-done | bytes 524304
  258.6 2.6 fusion.50
  261.2 80.9 %all-gather.9.cloned.1.call-done = bf16[8192,512]{1,0:T(8,128)(2,1)} async-done(((bf16[1024,512]{1,0:T(8,128)(2,1)}), bf16[8192,512]{1,0:T(8,128)(2,1)}) %all-gather.9.cloned.1.call-update) | async-done | bytes 8388624 | tf_op jit(solution)/shard_map/all_gather | solution.py:140
  342.2 5.2 %reduce_sum.65 = bf16[1024,512]{1,0:T(8,128)(2,1)S(1)} reduce(bf16[8,1024,512]{2,1,0:T(8,128)(2,1)} %bitcast.60, bf16[]{:T(256)} %constant.78.clone.1), dimensions={0}, to_apply=%region_8.0 | reduce | flops 3670016 | bytes 9437186 | tf_op jit(solution)/shard_map/reduce_sum | solution.py:140
  347.4 1.6 convert_element_type.175
  (89 shorter events, 17.2 us)
Async XLA Ops:
  7.2 51.1 %copy-start = (bf16[1024,512]{1,0:T(8,128)(2,1)S(1)}, bf16[1024,512]{1,0:T(8,128)(2,1)}, u32[]{:S(2)}) copy-start(bf16[1024,512]{1,0:T(8,128)(2,1)} %param.21) | copy-start | bytes 3145732
  7.2 2.7 copy-start.19
  7.2 47.8 %all-gather.5.cloned.1.call-start = ((), (), s32[]{:S(2)}) async-start(), calls=%async_computation.2 | async-start | bytes 2621440 | tf_op jit(solution)/shard_map/all_gather | solution.py:83
  13.9 4.0 %copy-start.23 = (s32[4,512]{1,0:T(4,128)S(1)}, s32[4,512]{1,0:T(4,128)}, u32[]{:S(2)}) copy-start(s32[4,512]{1,0:T(4,128)} %param.28) | copy-start | bytes 24580
  13.9 4.0 %copy-start.24 = (s32[4,512]{1,0:T(4,128)S(1)}, s32[4,512]{1,0:T(4,128)}, u32[]{:S(2)}) copy-start(s32[4,512]{1,0:T(4,128)} %param.29) | copy-start | bytes 24580
  13.9 4.0 %copy-start.21 = (s32[4,1024]{1,0:T(4,128)S(1)}, s32[4,1024]{1,0:T(4,128)}, u32[]{:S(2)}) copy-start(s32[4,1024]{1,0:T(4,128)} %param.27) | copy-start | bytes 49156
  13.9 4.0 %copy-start.22 = (s32[4,1024]{1,0:T(4,128)S(1)}, s32[4,1024]{1,0:T(4,128)}, u32[]{:S(2)}) copy-start(s32[4,1024]{1,0:T(4,128)} %param.30) | copy-start | bytes 49156
  13.9 41.0 %copy-start.8 = (bf16[1024,512]{1,0:T(8,128)(2,1)S(1)}, bf16[1024,512]{1,0:T(8,128)(2,1)}, u32[]{:S(2)}) copy-start(bf16[1024,512]{1,0:T(8,128)(2,1)} %param.23) | copy-start | bytes 3145732
  16.9 75.1 %all-gather.7.cloned.1.call-start = ((), (), s32[]{:S(2)}) async-start(), calls=%async_computation.3 | async-start | bytes 2621440 | tf_op jit(solution)/shard_map/all_gather | solution.py:106
  17.7 164.3 %all-reduce.5.cloned.1.call-start = ((), (), s32[]{:S(2)}) async-start(), calls=%async_computation.7 | async-start | bytes 6291456 | tf_op jit(solution)/shard_map/psum | solution.py:143
  55.0 3.3 copy-start.26
  92.0 4.0 %copy-start.4 = (bf16[4,256,1024]{2,1,0:T(8,128)(2,1)S(1)}, bf16[4,256,1024]{2,1,0:T(8,128)(2,1)}, u32[]{:S(2)}) copy-start(bf16[4,256,1024]{2,1,0:T(8,128)(2,1)} %all-gather.7.cloned.1.call-done) | copy-start | bytes 6291460
  92.0 4.0 %copy-start.12 = (bf16[512,1024]{1,0:T(8,128)(2,1)S(1)}, bf16[512,1024]{1,0:T(8,128)(2,1)}, u32[]{:S(2)}) copy-start(bf16[512,1024]{1,0:T(8,128)(2,1)} %param.26) | copy-start | bytes 3145732
  92.0 4.0 %copy-start.14 = (bf16[512,1024]{1,0:T(8,128)(2,1)S(1)}, bf16[512,1024]{1,0:T(8,128)(2,1)}, u32[]{:S(2)}) copy-start(bf16[512,1024]{1,0:T(8,128)(2,1)} %param.25) | copy-start | bytes 3145732
  99.6 3.1 copy-start.9
  99.6 3.1 copy-start.27
  105.0 115.6 %reduce-scatter.9.cloned.1.call-start = ((), (), s32[]{:S(2)}) async-start(), calls=%async_computation.6 | async-start | bytes 2621440
  105.2 2.7 copy-start.2
  105.3 2.7 copy-start.10
  105.3 2.7 copy-start.11
  110.6 148.0 %reduce-scatter.7.cloned.1.call-start = ((), (), s32[]{:S(2)}) async-start(), calls=%async_computation.5 | async-start | bytes 2621440
  116.1 226.1 %all-gather.9.cloned.1.call-start = ((), (), s32[]{:S(2)}) async-start(), calls=%async_computation.4 | async-start | bytes 9437184 | tf_op jit(solution)/shard_map/all_gather | solution.py:140
  182.0 2.9 copy-start.17
  186.5 72.2 %copy-start.7 = (bf16[1,256,1024]{2,1,0:T(8,128)(2,1)S(1)}, bf16[1,256,1024]{2,1,0:T(8,128)(2,1)}, u32[]{:S(2)}) copy-start(bf16[1,256,1024]{2,1,0:T(8,128)(2,1)} %param.31) | copy-start | bytes 1572868
  (10 other events, 17.9 us)
Sparse Core Ops, SparseCore 0:
  17.0 37.8 all-gather.4
  56.8 35.1 all-gather.6
  105.1 76.8 all-reduce.4
  185.4 35.1 reduce-scatter.8
  223.4 35.1 reduce-scatter.6
  260.1 82.0 all-gather.8
